TPU v7x, 32 devices: a whole 2x2x4 slice. The times are simulated.
32 devices in a mesh: seq: 8 (over z, x), head: 4 (over y, core).
Axes of the slice: x: 2, y: 2, z: 4, core: 2. Of those that a mesh axis runs over, the one named last changes fastest.
Arguments:
- tokens: bfloat16 [2048, 3584], P('seq'), may hold values from -16 to 16
- length: int32 [1], replicated, may hold values from 512 to 2048
- in_gain: float32 [3584], replicated, may hold values from 0.5 to 1.5
- q_weight: bfloat16 [3584, 3584], P(None, 'head'), may hold values from -0.09375 to 0.09375
- q_bias: float32 [3584], P('head'), may hold values from -60 to 60
- k_weight: bfloat16 [3584, 512], P(None, 'head'), may hold values from -0.09375 to 0.09375
- k_bias: float32 [512], P('head'), may hold values from -60 to 60
- v_weight: bfloat16 [3584, 512], P(None, 'head'), may hold values from -0.09375 to 0.09375
- v_bias: float32 [512], P('head'), may hold values from -2 to 2
- o_weight: bfloat16 [3584, 3584], P('head'), may hold values from -0.125 to 0.125
- final_gain: float32 [3584], P('head'), may hold values from 0.5 to 1.5
Outputs:
- hidden: bfloat16 [2048, 3584], P('seq', 'head')
- embedding: float32 [3584], P('head')
All inputs are finite; a program needn't handle non-finite values.
Results may differ from a plain program's by a relative error of at most 0.0075.
The roundings to bfloat16 on the way count: a program that leaves them out, or rounds other values in their place, can miss the bound.
Values may be sent and summed in bfloat16 or wider, within the bound.
A program may use at most 192 MiB of HBM per device.

v0:
```python
import jax
import jax.numpy as jnp
from jax import lax
from jax.sharding import PartitionSpec as P

D = 3584
HEAD_DIM = 128


rope_base = 1000000.0
epsilon = 1e-06


def rms_norm(inputs, gain):
    inputs = inputs.astype(jnp.float32)
    return inputs * lax.rsqrt(jnp.mean(inputs * inputs, axis=-1, keepdims=True) + epsilon) * gain


def rope_tables(positions):
    half_dim = HEAD_DIM // 2
    inverse = rope_base ** (-(jnp.arange(half_dim, dtype=jnp.float32) * 2.0) / HEAD_DIM)
    angles = positions.astype(jnp.float32)[:, None] * inverse[None, :]
    angles = jnp.concatenate([angles, angles], axis=1)
    return (jnp.cos(angles), jnp.sin(angles))


def rotate(inputs, cosine, sine):
    half_dim = HEAD_DIM // 2
    turned = jnp.concatenate([-inputs[..., half_dim:], inputs[..., :half_dim]], axis=-1)
    return inputs * cosine[:, None, :] + turned * sine[:, None, :]


def key_scores(queries, key_block):
    return lax.dot_general(
        queries, key_block, (((1,), (1,)), ((), ())), preferred_element_type=jnp.float32
    )


def body(
    tokens,
    length,
    in_gain,
    q_weight,
    q_bias,
    k_weight,
    k_bias,
    v_weight,
    v_bias,
    o_weight,
    final_gain,
):
    tok_rows = tokens.shape[0]
    head_count = q_weight.shape[1] // HEAD_DIM
    offset = lax.axis_index("seq") * tok_rows
    limit = length[0]
    positions = offset + jnp.arange(tok_rows, dtype=jnp.int32)
    normed = rms_norm(tokens, in_gain).astype(jnp.bfloat16)
    cosine, sine = rope_tables(positions)
    query = jnp.dot(normed, q_weight, preferred_element_type=jnp.float32) + q_bias
    query = rotate(query.reshape(tok_rows, head_count, HEAD_DIM), cosine, sine) * HEAD_DIM ** (-0.5)
    query = query.astype(jnp.bfloat16).reshape(tok_rows * head_count, HEAD_DIM)
    keys = jnp.dot(normed, k_weight, preferred_element_type=jnp.float32) + k_bias
    keys = (
        rotate(keys.reshape(tok_rows, 1, HEAD_DIM), cosine, sine)
        .astype(jnp.bfloat16)
        .reshape(tok_rows, HEAD_DIM)
    )
    values = (jnp.dot(normed, v_weight, preferred_element_type=jnp.float32) + v_bias).astype(
        jnp.bfloat16
    )
    q_rows = query.shape[0]

    def absorb(carry, piece):
        top, total, accum = carry
        k_piece, v_piece = piece
        count = k_piece.shape[0]
        live = jnp.arange(count, dtype=jnp.int32) < limit
        scores = jnp.where(live[None, :], key_scores(query, k_piece), -1e30)
        new_top = jnp.maximum(top, jnp.max(scores, axis=1))
        weights = jnp.where(live[None, :], jnp.exp(scores - new_top[:, None]), 0.0)
        total = jnp.sum(weights, axis=1)
        accum = jnp.dot(weights.astype(jnp.bfloat16), v_piece, preferred_element_type=jnp.float32)
        return (new_top, total, accum)

    initial = (
        jnp.full((q_rows,), -1e30, jnp.float32),
        jnp.zeros((q_rows,), jnp.float32),
        jnp.zeros((q_rows, HEAD_DIM), jnp.float32),
    )
    piece = (
        lax.all_gather(keys, "seq", axis=0, tiled=True),
        lax.all_gather(values, "seq", axis=0, tiled=True),
    )

    def update(state):
        return absorb(state, piece)

    def unchanged(state):
        return state

    top, total, accum = lax.cond(jnp.int32(0) < limit, update, unchanged, initial)
    attended = (
        (accum / total[:, None]).astype(jnp.bfloat16).reshape(tok_rows, head_count * HEAD_DIM)
    )
    mixed = jnp.dot(attended, o_weight, preferred_element_type=jnp.float32)
    width_share = D // lax.axis_size("head")
    column = lax.axis_index("head") * width_share
    shared = lax.psum_scatter(
        mixed.astype(jnp.bfloat16), "head", scatter_dimension=1, tiled=True
    ).astype(jnp.float32)
    hidden_full = (
        lax.dynamic_slice_in_dim(tokens, column, width_share, 1).astype(jnp.float32) + shared
    )
    squares = lax.psum(jnp.sum(hidden_full * hidden_full, axis=1), "head")
    final = hidden_full * lax.rsqrt(squares[:, None] / D + epsilon) * final_gain
    row_live = positions < limit
    local_sum = jnp.sum(jnp.where(row_live[:, None], final, 0.0), axis=0)
    pooled_sum = lax.psum(local_sum, "seq")
    mean = pooled_sum / limit.astype(jnp.float32)
    power = lax.psum(jnp.sum(mean * mean), "head")
    embedding = mean * lax.rsqrt(power / D + epsilon)
    return (hidden_full.astype(jnp.bfloat16), embedding)


def solution(mesh):
    in_specs = (
        P("seq", None),
        P(),
        P(),
        P(None, "head"),
        P("head"),
        P(None, "head"),
        P("head"),
        P(None, "head"),
        P("head"),
        P("head", None),
        P("head"),
    )
    out_specs = (P("seq", "head"), P("head"))
    return jax.shard_map(body, mesh=mesh, in_specs=in_specs, out_specs=out_specs, check_vma=False)
```

profile of v0, /device:TPU:0, one launch (start us, length us, event | category | flops | bytes accessed | tf_op | source)
XLA Modules:
  0.0 211.3 jit_solution(12068621012374544557)
XLA Ops:
  7.2 2.0 fusion.7
  9.3 6.5 %convolution_add_fusion = f32[256,896]{1,0:T(8,128)} fusion(bf16[3584,896]{1,0:T(8,128)(2,1)} %param.16, f32[896]{0:T(1024)} %param.17, bf16[256,3584]{1,0:T(8,128)(2,1)} %param.13, f32[3584]{0:T(1024)} %param.15, f32[256]{0:T(256)S(1)} %add_rsqrt_fusion.1), kind=kOutput, calls=%fused_computation.16 | convolution fusion | flops 1648066560 | bytes 9193984 | tf_op jit(solution)/shard_map/dot_general | solution.py:59
  15.7 2.6 %copy.23 = f32[256,896]{0,1:T(8,128)} copy(f32[256,896]{1,0:T(8,128)} %convolution_add_fusion) | data formatting | bytes 1835008 | tf_op jit(solution)/shard_map/add | solution.py:59
  18.3 2.2 %reshape.119 = f32[1792,128]{1,0:T(8,128)} reshape(f32[256,896]{1,0:T(8,128)} %convolution_add_fusion) | data formatting | bytes 1835008 | tf_op jit(solution)/shard_map/reshape | solution.py:60
  22.2 1.1 fusion.18
  23.5 33.5 %all_gather.6 = bf16[2048,128]{0,1:T(8,128)(2,1)S(1)} all-gather(bf16[256,128]{0,1:T(8,128)(2,1)} %get-tuple-element.38), channel_id=1, replica_groups=mesh['seq'=8,'head'=4] {'seq'}, dimensions={0}, use_global_device_ids=true | all-gather | bytes 589824 | tf_op jit(solution)/shard_map/all_gather | solution.py:91
  57.0 1.9 fusion.10
  58.9 33.4 %all_gather.7 = bf16[2048,128]{1,0:T(8,128)(2,1)} all-gather(bf16[256,128]{1,0:T(8,128)(2,1)S(1)} %fusion.10), channel_id=1, replica_groups=mesh['seq'=8,'head'=4] {'seq'}, dimensions={0}, use_global_device_ids=true | all-gather | bytes 589824 | tf_op jit(solution)/shard_map/all_gather | solution.py:92
  93.6 1.0 concatenate.28
  95.8 1.1 mul.134
  96.8 1.4 copy.25
  98.3 1.0 concatenate.29
  99.3 2.4 %fusion.13 = bf16[1792,128]{1,0:T(8,128)(2,1)S(1)} fusion(f32[1792,128]{1,0:T(8,128)} %mul.134, f32[1792,64]{1,0:T(8,128)} %concatenate.29, f32[1792,64]{1,0:T(8,128)} %concatenate.28, f32[1792,128]{1,0:T(8,128)S(1)} %copy-done.3, f32[1792,128]{1,0:T(8,128)} %mul.131), kind=kLoop, calls=%fused_computation.23 | loop fusion | flops 1376256 | bytes 4128768 | tf_op jit(solution)/shard_map/convert_element_type | solution.py:61
  101.7 22.9 %conditional.1 = (f32[1792]{0:T(1024)S(1)}, f32[1792,128]{1,0:T(8,128)S(1)}) conditional(s32[]{:T(128)} %convert_element_type.49, () %tuple.16, (s32[]{:T(128)}, bf16[1792,128]{1,0:T(8,128)(2,1)S(1)}, bf16[2048,128]{0,1:T(8,128)(2,1)S(1)}, bf16[2048,128]{1,0:T(8,128)(2,1)S(1)}) %tuple.32), branch_computations={%region_1.0_spmd, %region_2.5_spmd} | conditional | flops 1915748608 | bytes 46516244 | solution.py:101
  102.6 7.3 %select_reduce_fusion = (f32[1792]{0:T(1024)S(1)}, f32[1792,2048]{1,0:T(8,128)}) fusion(pred[2048]{0:T(1024)(128)(4,1)S(1)} %iota_compare_fusion, bf16[1792,128]{1,0:T(8,128)(2,1)S(1)} %get-tuple-element.9, bf16[2048,128]{0,1:T(8,128)(2,1)S(1)} %get-tuple-element.28), kind=kOutput, calls=%fused_computation.1 | convolution fusion | flops 946862336 | bytes 15672320 | tf_op jit(solution)/shard_map/cond/branch_1_fun/dot_general | solution.py:34
  109.9 8.2 %fusion.1 = f32[1792]{0:T(1024)S(1)} fusion(f32[1792,2048]{1,0:T(8,128)} %get-tuple-element.31, f32[1792]{0:T(1024)S(1)} %broadcast_maximum_fusion, pred[2048]{0:T(1024)(128)(4,1)S(1)} %iota_compare_fusion), kind=kLoop, calls=%fused_computation.3 | loop fusion | flops 14678272 | bytes 14696448 | tf_op jit(solution)/shard_map/cond/branch_1_fun/reduce_sum | solution.py:81
  118.0 6.6 %fusion.2 = f32[1792,128]{1,0:T(8,128)S(1)} fusion(bf16[2048,128]{1,0:T(8,128)(2,1)S(1)} %get-tuple-element.11, f32[1792,2048]{1,0:T(8,128)} %get-tuple-element.31, f32[1792]{0:T(1024)S(1)} %broadcast_maximum_fusion, pred[2048]{0:T(1024)(128)(4,1)S(1)} %iota_compare_fusion), kind=kOutput, calls=%fused_computation.4 | convolution fusion | flops 954204160 | bytes 16131072 | tf_op jit(solution)/shard_map/cond/branch_1_fun/dot_general | solution.py:82
  125.4 6.1 %convolution_convert_fusion = bf16[256,3584]{1,0:T(8,128)(2,1)} fusion(bf16[256,896]{1,0:T(8,128)(2,1)S(1)} %reshape.122, bf16[896,3584]{1,0:T(8,128)(2,1)} %param.22), kind=kOutput, calls=%fused_computation.10 | convolution fusion | flops 1645084672 | bytes 8716288 | tf_op jit(solution)/shard_map/dot_general | solution.py:105
  131.6 4.0 %copy.29 = bf16[256,3584]{0,1:T(8,128)(2,1)} copy(bf16[256,3584]{1,0:T(8,128)(2,1)} %convolution_convert_fusion) | data formatting | bytes 3670016
  135.6 30.9 %reduce-scatter.4.cloned.1.call-done = bf16[896,256]{1,0:T(8,128)(2,1)} async-done(((bf16[3584,256]{1,0:T(8,128)(2,1)}), bf16[896,256]{1,0:T(8,128)(2,1)}) %reduce-scatter.4.cloned.1.call-update) | async-done | bytes 458768
  166.5 1.3 copy.30
  168.0 5.8 %psum.21 = f32[256]{0:T(256)S(1)} all-reduce(f32[256]{0:T(256)S(1)} %multiply_reduce_fusion), channel_id=1, replica_groups=mesh['seq'=8,'head'=4] {'head'}, use_global_device_ids=true, to_apply=%region_7.8 | all-reduce | flops 256 | bytes 2048 | tf_op jit(solution)/shard_map/psum | solution.py:114
  174.8 21.5 %psum.22 = f32[896]{0:T(1024)S(1)} all-reduce(f32[896]{0:T(1024)S(1)} %get-tuple-element.32), channel_id=1, replica_groups=mesh['seq'=8,'head'=4] {'seq'}, use_global_device_ids=true, to_apply=%region_9.10 | all-reduce | flops 896 | bytes 7168 | tf_op jit(solution)/shard_map/psum | solution.py:118
  196.9 6.3 %psum.23 = f32[]{:T(128)} all-reduce(f32[]{:T(128)} %multiply_reduce_fusion.1), channel_id=1, replica_groups=mesh['seq'=8,'head'=4] {'head'}, use_global_device_ids=true, to_apply=%region_11.12 | all-reduce | flops 1 | bytes 8 | tf_op jit(solution)/shard_map/psum | solution.py:120
  (45 shorter events, 7.6 us)
Async XLA Ops:
  7.2 14.0 %copy-start = (bf16[3584,128]{1,0:T(8,128)(2,1)S(1)}, bf16[3584,128]{1,0:T(8,128)(2,1)}, u32[]{:S(2)}) copy-start(bf16[3584,128]{1,0:T(8,128)(2,1)} %param.18) | copy-start | bytes 2752516
  7.2 159.3 %reduce-scatter.4.cloned.1.call-start = ((), (), s32[]{:S(2)}) async-start(), calls=%async_computation.1 | async-start | bytes 2293760
  15.7 5.4 %copy-start.1 = (bf16[256,3584]{1,0:T(8,128)(2,1)S(1)}, bf16[256,3584]{1,0:T(8,128)(2,1)}, u32[]{:S(2)}) copy-start(bf16[256,3584]{1,0:T(8,128)(2,1)} %param.13) | copy-start | bytes 5505028
  15.7 5.5 %copy-start.7 = (f32[3584]{0:T(1024)S(1)}, f32[3584]{0:T(1024)}, u32[]{:S(2)}) copy-start(f32[3584]{0:T(1024)} %param.15) | copy-start | bytes 43012
  15.7 5.5 %copy-start.8 = (f32[128]{0:T(128)S(1)}, f32[128]{0:T(128)}, u32[]{:S(2)}) copy-start(f32[128]{0:T(128)} %param.19) | copy-start | bytes 1540
  18.3 38.7 %copy-start.9 = (f32[128]{0:T(128)S(1)}, f32[128]{0:T(128)}, u32[]{:S(2)}) copy-start(f32[128]{0:T(128)} %param.21) | copy-start | bytes 1540
  23.5 68.8 %copy-start.4 = (f32[256,896]{0,1:T(8,128)S(1)}, f32[256,896]{0,1:T(8,128)}, u32[]{:S(2)}) copy-start(f32[256,896]{0,1:T(8,128)} %copy.23) | copy-start | bytes 2752516
  95.7 3.6 %copy-start.3 = (f32[1792,128]{1,0:T(8,128)S(1)}, f32[1792,128]{1,0:T(8,128)}, u32[]{:S(2)}) copy-start(f32[1792,128]{1,0:T(8,128)} %reshape.119) | copy-start | bytes 2752516
  99.3 2.4 %copy-start.5 = (bf16[2048,128]{1,0:T(8,128)(2,1)S(1)}, bf16[2048,128]{1,0:T(8,128)(2,1)}, u32[]{:S(2)}) copy-start(bf16[2048,128]{1,0:T(8,128)(2,1)} %all_gather.7) | copy-start | bytes 1572868
  131.6 36.2 %copy-start.2 = (bf16[256,3584]{1,0:T(8,128)(2,1)S(1)}, bf16[256,3584]{1,0:T(8,128)(2,1)}, u32[]{:S(2)}) copy-start(bf16[256,3584]{1,0:T(8,128)(2,1)} %param.13) | copy-start | bytes 5505028
  131.6 42.2 %copy-start.6 = (f32[896]{0:T(1024)S(1)}, f32[896]{0:T(1024)}, u32[]{:S(2)}) copy-start(f32[896]{0:T(1024)} %param.23) | copy-start | bytes 10756
Sparse Core Ops, SparseCore 0:
  135.7 30.7 reduce-scatter.3
where the time goes:
time: 212 us; the launch traced here: 211 us
  blocking collectives  100 us (47%)
  waiting for transfers between devices  30.9 us (15%)
  matrix products  29.3 us (14%)
  other arithmetic  18.1 us (9%)
  local copies, waits for them, and re-layouts  16.8 us (8%)
  between operations  15.6 us (7%)
    all_gather x1, blocking collectives, body(): lax.all_gather(keys, 'seq', axis=0, tiled=True)  33.5 us
    all_gather x1, blocking collectives, body(): lax.all_gather(values, 'seq', axis=0, tiled=True)  33.4 us
    unnamed x2, waiting for transfers between devices  30.9 us
    psum x1, blocking collectives, body(): pooled_sum = lax.psum(local_sum, 'seq')  21.5 us
    reduce_sum x1, other arithmetic, absorb(): total = jnp.sum(weights, axis=1)  8.15 us
    dot_general x1, matrix products, key_scores(): lax.dot_general(queries, key_block, (((1,), (1,)), ((), ())), preferred_e...  7.28 us
    dot_general x1, matrix products, absorb(): jnp.dot(weights.astype(jnp.bfloat16), v_piece, preferred_element_type=jnp...  6.61 us
    dot_general x1, matrix products, body(): jnp.dot(normed, q_weight, preferred_element_type=jnp.float32) + q_bias  6.46 us
  transfers between devices with their start and end apart: 1, of which 1 were waited for; matrix products, arithmetic and copies ran while one was open for 0% of the time, Pallas kernels for 0%

commit v1 on v0

v1 whole, which is shorter than its diff:
```python
import functools

import jax
import jax.numpy as jnp
import numpy as np
from jax import lax
from jax.experimental import pallas as pl
from jax.experimental.pallas import tpu as pltpu
from jax.sharding import PartitionSpec as P

HEAD_DIM = 128
ROPE_BASE = 1000000.0
EPS = 1e-06
MESH = pl.DeviceIdType.MESH
F32 = jnp.float32
BF16 = jnp.bfloat16
LOW = -1e30


def widths(share):
    out, at = [], 0
    first = share % 256 or 256
    while at < share:
        width = first if at == 0 else 256
        out.append((at, width))
        at += width
    return out


def dot(a, b):
    return jnp.dot(a, b, preferred_element_type=F32)


def kernel(
    n_seq,
    n_head,
    length_ref,
    tokens_hbm,
    gain_ref,
    wq_hbm,
    qb_ref,
    wk_hbm,
    kb_ref,
    wv_hbm,
    vb_ref,
    wo_hbm,
    fgain_ref,
    cos_row,
    sin_row,
    cos_off,
    sin_off,
    hidden_hbm,
    emb_ref,
    tok,
    normed,
    wkv,
    wq,
    wo,
    cos,
    sin,
    qt,
    kbuf,
    vbuf,
    m_ref,
    l_ref,
    acc_ref,
    att,
    hid,
    hid_bf,
    sqbuf,
    pbuf,
    wbuf,
    local_sem,
    ring_send,
    ring_recv,
    pair_send,
    pair_recv,
    cross_send,
    cross_recv,
    sq_send,
    sq_recv,
    pool_send,
    pool_recv,
    pow_send,
    pow_recv,
    *chunk_bufs,
):
    rows, width = tok.shape
    share = hid.shape[1]
    heads = qt.shape[0]
    half = n_seq // 2
    n_y = n_head // 2
    chunks = widths(share)
    psend, precv = chunk_bufs[0::5], chunk_bufs[1::5]
    pown, ysend, yrecv = chunk_bufs[2::5], chunk_bufs[3::5], chunk_bufs[4::5]
    ms = lax.axis_index("seq")
    mh = lax.axis_index("head")
    limit = length_ref[0]

    loads = [
        pltpu.make_async_copy(tokens_hbm, tok, local_sem.at[0]),
        pltpu.make_async_copy(wk_hbm, wkv.at[:, :HEAD_DIM], local_sem.at[1]),
        pltpu.make_async_copy(wv_hbm, wkv.at[:, HEAD_DIM:], local_sem.at[2]),
        pltpu.make_async_copy(wq_hbm, wq, local_sem.at[3]),
        pltpu.make_async_copy(wo_hbm, wo, local_sem.at[4]),
    ]
    for load in loads:
        load.start()

    barrier = pltpu.get_barrier_semaphore()

    def greet(d, carry):
        pl.semaphore_signal(
            barrier, inc=1, device_id={"seq": lax.rem(ms + d, n_seq)}, device_id_type=MESH
        )
        return carry

    lax.fori_loop(1, n_seq, greet, 0)
    for d in range(1, n_head):
        pl.semaphore_signal(
            barrier, inc=1, device_id={"head": lax.rem(mh + d, n_head)}, device_id_type=MESH
        )

    far = pl.ds(pl.multiple_of(ms * 8, 8), 8)
    co, so = cos_off[far, :][:1], sin_off[far, :][:1]
    lane = lax.broadcasted_iota(jnp.int32, (1, HEAD_DIM), 1)
    sign = jnp.where(lane < HEAD_DIM // 2, -1.0, 1.0)
    cos[...] = cos_row[...] * co - sin_row[...] * so
    sin[...] = (sin_row[...] * co + cos_row[...] * so) * sign

    def rope(u):
        return u * cos[...] + pltpu.roll(u, HEAD_DIM // 2, 1) * sin[...]

    loads[0].wait()
    block = 16

    def norm_block(i, carry):
        at = pl.ds(pl.multiple_of(i * block, block), block)
        x = tok[at, :].astype(F32)
        mean = jnp.sum(x * x, axis=1, keepdims=True) / width
        normed[at, :] = (x * lax.rsqrt(mean + EPS) * gain_ref[...]).astype(BF16)
        return carry

    lax.fori_loop(0, rows // block, norm_block, 0)

    loads[1].wait()
    loads[2].wait()
    kv = dot(normed[...], wkv[...])
    kbuf[ms] = rope(kv[:, :HEAD_DIM] + kb_ref[...]).astype(BF16)
    vbuf[ms] = jnp.transpose(kv[:, HEAD_DIM:] + vb_ref[...]).astype(BF16)

    q2 = lax.div(ms, 2)
    pos = q2 + (ms - 2 * q2) * (n_seq - 1 - 2 * q2)

    def slot(p):
        p = lax.rem(p + 2 * n_seq, n_seq)
        back = lax.div(p, half)
        return (1 - back) * 2 * p + back * (2 * (n_seq - 1 - p) + 1)

    ends = (slot(pos + 1), slot(pos - 1))

    def moved(way, kind, s, hops):
        sign_of = 1 if way == 0 else -1
        at = slot(pos - sign_of * hops)
        buf = vbuf if kind else kbuf
        return pltpu.make_async_remote_copy(
            src_ref=buf.at[at],
            dst_ref=buf.at[at],
            send_sem=ring_send.at[2 * way + kind, s],
            recv_sem=ring_recv.at[2 * way + kind, s],
            device_id={"seq": ends[way]},
            device_id_type=MESH,
        )

    def send(way, kind, s):
        return moved(way, kind, s, s - 1)

    def arrival(way, kind, s):
        return moved(way, kind, s, s)

    pl.semaphore_wait(barrier, n_seq + n_head - 2)
    for kind in (0, 1):
        for way in (0, 1):
            send(way, kind, 1).start()

    def put_query(h, u):
        at = pl.ds(pl.multiple_of(h * HEAD_DIM, HEAD_DIM), HEAD_DIM)
        u = rope(u + qb_ref[:, at]) * HEAD_DIM ** (-0.5)
        qt[h] = jnp.transpose(u).astype(BF16)

    loads[3].wait()

    def query_pair(j, carry):
        at = pl.ds(pl.multiple_of(j * 2 * HEAD_DIM, 2 * HEAD_DIM), 2 * HEAD_DIM)
        u = dot(normed[...], wq[:, at])
        put_query(2 * j, u[:, :HEAD_DIM])
        put_query(2 * j + 1, u[:, HEAD_DIM:])
        return carry

    lax.fori_loop(0, heads // 2, query_pair, 0)
    if heads % 2:
        put_query(heads - 1, dot(normed[...], wq[:, (heads - 1) * HEAD_DIM :]))

    def attend(blocks, first):
        def per_head(h, carry):
            query = qt[h]
            scores = []
            for b in blocks:
                s = dot(kbuf[b], query)
                key_at = b * rows + lax.broadcasted_iota(jnp.int32, (rows, 1), 0)
                scores.append(jnp.where(key_at < limit, s, LOW))
            tops = [jnp.max(s, axis=0, keepdims=True) for s in scores]
            top = functools.reduce(jnp.maximum, tops)
            if not first:
                old = m_ref[h][:1]
                top = jnp.maximum(old, top)
                alpha = jnp.exp(old - top)
            total, mixed = None, None
            for b, s in zip(blocks, scores):
                p = jnp.exp(s - top)
                part = jnp.sum(p, axis=0, keepdims=True)
                prod = dot(vbuf[b], p.astype(BF16))
                total = part if total is None else total + part
                mixed = prod if mixed is None else mixed + prod
            if not first:
                total = total + l_ref[h][:1] * alpha
                mixed = mixed + acc_ref[h] * alpha
            m_ref[h] = jnp.broadcast_to(top, (8, rows))
            l_ref[h] = jnp.broadcast_to(total, (8, rows))
            acc_ref[h] = mixed
            return carry

        lax.fori_loop(0, heads, per_head, 0)

    def forward(s, kinds_ways):
        for kind in (0, 1):
            for way in (0, 1):
                arrival(way, kind, s).wait_recv()
                if (way, kind) in kinds_ways:
                    send(way, kind, s + 1).start()

    every = ((0, 0), (0, 1), (1, 0), (1, 1))
    last = ((0, 0), (1, 1))
    forward(1, every if half > 2 else last)
    attend([ms], True)
    attend([slot(pos - 1), slot(pos + 1)], False)

    def ring_step(s, carry):
        forward(s, every)
        attend([slot(pos - s), slot(pos + s)], False)
        return carry

    if half > 3:
        lax.fori_loop(2, half - 1, ring_step, 0)
    if half > 2:
        forward(half - 1, last)
        attend([slot(pos - half + 1), slot(pos + half - 1)], False)
    for way, kind in last:
        arrival(way, kind, half).wait_recv()
    attend([slot(pos - half)], False)

    def finish(h, carry):
        at = pl.ds(pl.multiple_of(h * HEAD_DIM, HEAD_DIM), HEAD_DIM)
        att[:, at] = jnp.transpose(acc_ref[h] / l_ref[h][:1]).astype(BF16)
        return carry

    lax.fori_loop(0, heads, finish, 0)

    loads[4].wait()
    my = lax.div(mh, 2)
    mc = mh - 2 * my
    partner = 2 * my + 1 - mc

    def partial(dest, at, wide):
        cols = pl.ds(pl.multiple_of(dest * share + at, HEAD_DIM), wide)
        return dot(att[...], wo[:, cols])

    def pair_copy(i):
        return pltpu.make_async_remote_copy(
            src_ref=psend[i],
            dst_ref=precv[i],
            send_sem=pair_send.at[i],
            recv_sem=pair_recv.at[i],
            device_id={"head": partner},
            device_id_type=MESH,
        )

    def cross_copy(i, d):
        return pltpu.make_async_remote_copy(
            src_ref=ysend[i].at[d - 1],
            dst_ref=yrecv[i].at[d - 1],
            send_sem=cross_send.at[i, d - 1],
            recv_sem=cross_recv.at[i, d - 1],
            device_id={"head": 2 * lax.rem(my + d, n_y) + mc},
            device_id_type=MESH,
        )

    def to_partner(i):
        at, wide = chunks[i]
        for y in range(n_y):
            psend[i][y] = partial(2 * y + 1 - mc, at, wide).astype(BF16)
        pair_copy(i).start()
        for d in range(1, n_y):
            pown[i][d] = partial(2 * lax.rem(my + d, n_y) + mc, at, wide)

    def across(i):
        pair_copy(i).wait_recv()
        for d in range(1, n_y):
            y = lax.rem(my + d, n_y)
            ysend[i][d - 1] = (pown[i][d] + precv[i][y].astype(F32)).astype(BF16)
            cross_copy(i, d).start()

    for i in range(len(chunks)):
        to_partner(i)
        if i:
            across(i - 1)
    across(len(chunks) - 1)
    for i, (at, wide) in enumerate(chunks):
        pown[i][0] = partial(mh, at, wide)

    squares = None
    outs = []
    for i, (at, wide) in enumerate(chunks):
        mine = pl.ds(pl.multiple_of(mh * share + at, HEAD_DIM), wide)
        base = tok[:, mine].astype(F32) + (pown[i][0] + precv[i][my].astype(F32))
        for d in range(1, n_y):
            cross_copy(i, d).wait_recv()
            base = base + yrecv[i][d - 1].astype(F32)
        hid[:, at : at + wide] = base
        hid_bf[:, at : at + wide] = base.astype(BF16)
        for g in range(0, wide, HEAD_DIM):
            piece = base[:, g : g + HEAD_DIM]
            squares = piece * piece if squares is None else squares + piece * piece
    out_copy = pltpu.make_async_copy(hid_bf, hidden_hbm, local_sem.at[5])
    out_copy.start()

    def head_copy(buf, send_sems, recv_sems, d):
        return pltpu.make_async_remote_copy(
            src_ref=buf.at[mh],
            dst_ref=buf.at[mh],
            send_sem=send_sems.at[d - 1],
            recv_sem=recv_sems.at[d - 1],
            device_id={"head": lax.rem(mh + d, n_head)},
            device_id_type=MESH,
        )

    def head_arrival(buf, send_sems, recv_sems, d):
        source = lax.rem(mh + n_head - d, n_head)
        return pltpu.make_async_remote_copy(
            src_ref=buf.at[source],
            dst_ref=buf.at[source],
            send_sem=send_sems.at[d - 1],
            recv_sem=recv_sems.at[d - 1],
            device_id={"head": source},
            device_id_type=MESH,
        )

    def head_sum(buf, send_sems, recv_sems, value):
        buf[mh] = jnp.broadcast_to(value, buf.shape[1:])
        for d in range(1, n_head):
            head_copy(buf, send_sems, recv_sems, d).start()
        for d in range(1, n_head):
            head_arrival(buf, send_sems, recv_sems, d).wait_recv()
        return functools.reduce(lambda a, b: a + b, [buf[d][:1] for d in range(n_head)])

    square_row = jnp.sum(jnp.transpose(squares), axis=0, keepdims=True)
    power = head_sum(sqbuf, sq_send, sq_recv, square_row)
    place = ms * rows + lax.broadcasted_iota(jnp.int32, (1, rows), 1)
    scale = jnp.where(place < limit, lax.rsqrt(power / width + EPS), 0.0)
    scale = jnp.transpose(jnp.broadcast_to(scale, (HEAD_DIM, rows)))

    groups = pbuf.shape[1]
    sums = []
    for g in range(0, share, HEAD_DIM):
        at = slice(g, g + HEAD_DIM)
        sums.append(jnp.sum(hid[:, at] * scale, axis=0, keepdims=True) * fgain_ref[:, at])
    sums += [jnp.zeros((1, HEAD_DIM), F32)] * (groups - len(sums))
    pbuf[ms] = jnp.concatenate(sums, axis=0)

    def pool_copy(d):
        return pltpu.make_async_remote_copy(
            src_ref=pbuf.at[ms],
            dst_ref=pbuf.at[ms],
            send_sem=pool_send.at[d - 1],
            recv_sem=pool_recv.at[d - 1],
            device_id={"seq": lax.rem(ms + d, n_seq)},
            device_id_type=MESH,
        )

    def pool_start(d, carry):
        pool_copy(d).start()
        return carry

    def pool_wait(d, carry):
        source = lax.rem(ms + n_seq - d, n_seq)
        pltpu.make_async_remote_copy(
            src_ref=pbuf.at[source],
            dst_ref=pbuf.at[source],
            send_sem=pool_send.at[d - 1],
            recv_sem=pool_recv.at[d - 1],
            device_id={"seq": source},
            device_id_type=MESH,
        ).wait_recv()
        return carry

    lax.fori_loop(1, n_seq, pool_start, 0)
    lax.fori_loop(1, n_seq, pool_wait, 0)
    mean = functools.reduce(lambda a, b: a + b, [pbuf[d] for d in range(n_seq)])
    mean = mean / limit.astype(F32)
    total = head_sum(wbuf, pow_send, pow_recv, jnp.sum(mean * mean, axis=0, keepdims=True))
    pooled = mean * lax.rsqrt(jnp.sum(total, axis=1, keepdims=True) / width + EPS)
    for g in range(share // HEAD_DIM):
        emb_ref[:, g * HEAD_DIM : (g + 1) * HEAD_DIM] = pooled[g : g + 1]

    def sent(s, carry):
        for way, kind in every:
            send(way, kind, s).wait_send()
        return carry

    lax.fori_loop(1, half, sent, 0)
    for way, kind in last:
        send(way, kind, half).wait_send()
    for i in range(len(chunks)):
        pair_copy(i).wait_send()
        for d in range(1, n_y):
            cross_copy(i, d).wait_send()
    for d in range(1, n_head):
        head_copy(sqbuf, sq_send, sq_recv, d).wait_send()
        head_copy(wbuf, pow_send, pow_recv, d).wait_send()

    def pool_sent(d, carry):
        pool_copy(d).wait_send()
        return carry

    lax.fori_loop(1, n_seq, pool_sent, 0)
    out_copy.wait()


def body(
    n_seq,
    n_head,
    tokens,
    length,
    in_gain,
    q_weight,
    q_bias,
    k_weight,
    k_bias,
    v_weight,
    v_bias,
    o_weight,
    final_gain,
):
    rows, width = tokens.shape
    share = width // n_head
    heads = q_weight.shape[1] // HEAD_DIM
    half = n_seq // 2
    n_y = n_head // 2
    inverse = ROPE_BASE ** (-(np.arange(HEAD_DIM // 2) * 2.0) / HEAD_DIM)
    inverse = np.concatenate([inverse, inverse])[None, :]
    near = np.arange(rows)[:, None] * inverse
    far = np.repeat(np.arange(n_seq) * rows, 8)[:, None] * inverse
    tables = [f(a).astype(np.float32) for a in (near, far) for f in (np.cos, np.sin)]

    chunks = widths(share)
    groups = -(-share // (8 * HEAD_DIM)) * 8
    chunk_bufs = []
    for _, wide in chunks:
        chunk_bufs += [
            pltpu.VMEM((n_y, rows, wide), BF16),
            pltpu.VMEM((n_y, rows, wide), BF16),
            pltpu.VMEM((n_y, rows, wide), F32),
            pltpu.VMEM((n_y - 1, rows, wide), BF16),
            pltpu.VMEM((n_y - 1, rows, wide), BF16),
        ]
    dma = pltpu.SemaphoreType.DMA
    hbm = pl.BlockSpec(memory_space=pl.ANY)
    vmem = pl.BlockSpec(memory_space=pltpu.VMEM)
    smem = pl.BlockSpec(memory_space=pltpu.SMEM)
    hidden, embedding = pl.pallas_call(
        functools.partial(kernel, n_seq, n_head),
        out_shape=(
            jax.ShapeDtypeStruct((rows, share), BF16),
            jax.ShapeDtypeStruct((1, share), F32),
        ),
        in_specs=[smem, hbm, vmem, hbm, vmem, hbm, vmem, hbm, vmem, hbm] + [vmem] * 5,
        out_specs=(hbm, vmem),
        scratch_shapes=[
            pltpu.VMEM((rows, width), BF16),
            pltpu.VMEM((rows, width), BF16),
            pltpu.VMEM((width, 2 * HEAD_DIM), BF16),
            pltpu.VMEM(q_weight.shape, BF16),
            pltpu.VMEM(o_weight.shape, BF16),
            pltpu.VMEM((rows, HEAD_DIM), F32),
            pltpu.VMEM((rows, HEAD_DIM), F32),
            pltpu.VMEM((heads, HEAD_DIM, rows), BF16),
            pltpu.VMEM((n_seq, rows, HEAD_DIM), BF16),
            pltpu.VMEM((n_seq, HEAD_DIM, rows), BF16),
            pltpu.VMEM((heads, 8, rows), F32),
            pltpu.VMEM((heads, 8, rows), F32),
            pltpu.VMEM((heads, HEAD_DIM, rows), F32),
            pltpu.VMEM((rows, heads * HEAD_DIM), BF16),
            pltpu.VMEM((rows, share), F32),
            pltpu.VMEM((rows, share), BF16),
            pltpu.VMEM((n_head, 8, rows), F32),
            pltpu.VMEM((n_seq, groups, HEAD_DIM), F32),
            pltpu.VMEM((n_head, 8, HEAD_DIM), F32),
            dma((6,)),
            dma((4, half + 1)),
            dma((4, half + 1)),
            dma((len(chunks),)),
            dma((len(chunks),)),
            dma((len(chunks), n_y)),
            dma((len(chunks), n_y)),
            dma((n_head,)),
            dma((n_head,)),
            dma((n_seq,)),
            dma((n_seq,)),
            dma((n_head,)),
            dma((n_head,)),
        ]
        + chunk_bufs,
        compiler_params=pltpu.CompilerParams(
            collective_id=0, has_side_effects=True, vmem_limit_bytes=60 * 1024 * 1024
        ),
    )(
        length,
        tokens,
        in_gain[None, :],
        q_weight,
        q_bias[None, :],
        k_weight,
        k_bias[None, :],
        v_weight,
        v_bias[None, :],
        o_weight,
        final_gain[None, :],
        *tables,
    )
    return hidden, embedding[0]


def solution(mesh):
    in_specs = (
        P("seq", None),
        P(),
        P(),
        P(None, "head"),
        P("head"),
        P(None, "head"),
        P("head"),
        P(None, "head"),
        P("head"),
        P("head", None),
        P("head"),
    )
    out_specs = (P("seq", "head"), P("head"))
    step = functools.partial(body, mesh.shape["seq"], mesh.shape["head"])
    return jax.shard_map(step, mesh=mesh, in_specs=in_specs, out_specs=out_specs, check_vma=False)
```

time: 212 us -> 65.7 us (0.31)
  blocking collectives: 100 us -> 0 us
  Pallas kernels: 0 us -> 57.1 us
  waiting for transfers between devices: 30.9 us -> 0 us
  matrix products: 29.3 us -> 0 us
  other arithmetic: 18.1 us -> 1.29 us
  between operations: 15.6 us -> 1.29 us
  local copies, waits for them, and re-layouts: 16.8 us -> 5.69 us
    all_gather x2 -> x0, blocking collectives: 66.9 us -> none  [the longest x1 33.5 us: body(): lax.all_gather(keys, 'seq', axis=0, tiled=True)]
    pallas_call x0 -> x1, Pallas kernels: none -> 57.1 us  [body(): pl.pallas_call(functools.partial(kernel, n_seq, n_head), out_shape=(jax.S...]
    psum x3 -> x0, blocking collectives: 33.6 us -> none  [the longest x1 21.5 us: body(): pooled_sum = lax.psum(local_sum, 'seq')]
    unnamed x2 -> x0, waiting for transfers between devices: 30.9 us -> none
    dot_general x6 -> x0, matrix products: 29.3 us -> none  [the longest x1 7.28 us: key_scores(): lax.dot_general(queries, key_block, (((1,), (1,)), ((), ())), preferred_e...]
    reduce_sum x5 -> x0, other arithmetic: 12 us -> none  [the longest x1 8.15 us: absorb(): total = jnp.sum(weights, axis=1)]
    broadcast_in_dim x0 -> x3, local copies, waits for them, and re-layouts: none -> 3.87 us  [the longest x1 1.33 us: body(): in_gain[None, :]]
    convert_element_type x4 -> x0, other arithmetic: 3.85 us -> none  [the longest x1 2.41 us: body(): query = query.astype(jnp.bfloat16).reshape(tok_rows * head_count, HEAD_DIM)]
  transfers between devices with their start and end apart: 1 -> 0, of which waited for: 1 -> 0; matrix products, arithmetic and copies ran while one was open for 0% -> 0% of each run, Pallas kernels for 0% -> 0%
where the time goes in v1:
time: 65.7 us; the launch traced here: 65.4 us
  Pallas kernels  57.1 us (87%)
  local copies, waits for them, and re-layouts  5.69 us (9%)
  other arithmetic  1.29 us (2%)
  between operations  1.29 us (2%)
    pallas_call x1, Pallas kernels, body(): pl.pallas_call(functools.partial(kernel, n_seq, n_head), out_shape=(jax.S...  57.1 us
    unnamed x1, local copies, waits for them, and re-layouts  1.82 us
    broadcast_in_dim x1, local copies, waits for them, and re-layouts, body(): in_gain[None, :]  1.33 us

profile of v1, /device:TPU:0, one launch (start us, length us, event | category | flops | bytes accessed | tf_op | source)
XLA Modules:
  0.0 65.4 jit_solution(7762628019749593125)
XLA Ops:
  1.3 1.3 %broadcast_in_dim.16.qb_ref = f32[1,896]{1,0:T(1,128)} reshape(f32[896]{0:T(1024)} %param.19) | data formatting | bytes 7168 | tf_op jit(solution)/shard_map/broadcast_in_dim | solution.py:531
  2.5 1.3 %broadcast_in_dim.19.fgain_ref = f32[1,896]{1,0:T(1,128)} reshape(f32[896]{0:T(1024)} %param.25) | data formatting | bytes 7168 | tf_op jit(solution)/shard_map/broadcast_in_dim | solution.py:537
  3.8 1.3 %broadcast_in_dim.15.gain_ref = f32[1,3584]{1,0:T(1,128)} reshape(f32[3584]{0:T(1024)} %param.17) | data formatting | bytes 28672 | tf_op jit(solution)/shard_map/broadcast_in_dim | solution.py:529
  5.1 57.1 %shard_map.158 = (bf16[256,896]{1,0:T(8,128)(2,1)}, f32[1,896]{1,0:T(1,128)}) custom-call(s32[1]{0:T(128)S(6)} %copy.18.length_ref, bf16[256,3584]{1,0:T(8,128)(2,1)} %tokens_hbm.1, f32[1,3584]{1,0:T(1,128)} %broadcast_in_dim.15.gain_ref, bf16[3584,896]{1,0:T(8,128)(2,1)} %wq_hbm.1, f32[1,896]{1,0:T(1,128)} %broadcast_in_dim.16.qb_ref, ...), custom_call_target="tpu_custom_call" | custom-call | tf_op jit(solution)/shard_map/pallas_call | solution.py:480
  62.3 1.3 %reduce = f32[896]{0:T(1024)} reduce(f32[1,896]{1,0:T(1,128)} %get-tuple-element.5, f32[]{:T(128)} %constant.12), dimensions={0}, to_apply=%get-tuple-element.5.reduce_sub_computation | reduce | bytes 7172 | tf_op jit(solution)/shard_map/pallas_call | solution.py:480
  63.6 1.8 %copy.19 = bf16[256,896]{1,0:T(8,128)(2,1)} copy(bf16[256,896]{1,0:T(8,128)(2,1)} %get-tuple-element.8) | data formatting | bytes 917504

commit v2 on v1

--- a/solution.py
+++ b/solution.py
@@ -22,9 +22,10 @@
     first = share % 256 or 256
     while at < share:
         width = first if at == 0 else 256
-        out.append((at, width))
+        out.append((1, at, width))
         at += width
-    return out
+    cut = out[len(out) // 2][1]
+    return [(0, 0, cut), (0, cut, share - cut)] + out
 
 
 def dot(a, b):
@@ -36,21 +37,26 @@
     n_head,
     length_ref,
     tokens_hbm,
-    gain_ref,
+    gain_1d,
     wq_hbm,
-    qb_ref,
+    qb_1d,
     wk_hbm,
-    kb_ref,
+    kb_1d,
     wv_hbm,
-    vb_ref,
+    vb_1d,
     wo_hbm,
-    fgain_ref,
+    fgain_1d,
     cos_row,
     sin_row,
     cos_off,
     sin_off,
     hidden_hbm,
     emb_ref,
+    gain_ref,
+    qb_ref,
+    kb_ref,
+    vb_ref,
+    fgain_ref,
     tok,
     normed,
     wkv,
@@ -87,7 +93,8 @@
 ):
     rows, width = tok.shape
     share = hid.shape[1]
-    heads = qt.shape[0]
+    heads = qt.shape[2] // (rows // 2)
+    part_rows = rows // 2
     half = n_seq // 2
     n_y = n_head // 2
     chunks = widths(share)
@@ -104,8 +111,18 @@
         pltpu.make_async_copy(wq_hbm, wq, local_sem.at[3]),
         pltpu.make_async_copy(wo_hbm, wo, local_sem.at[4]),
     ]
-    for load in loads:
+    for load in loads[:4]:
         load.start()
+
+    for flat, row in (
+        (gain_1d, gain_ref),
+        (qb_1d, qb_ref),
+        (kb_1d, kb_ref),
+        (vb_1d, vb_ref),
+        (fgain_1d, fgain_ref),
+    ):
+        for g in range(0, row.shape[1], HEAD_DIM):
+            row[:, g : g + HEAD_DIM] = flat[g : g + HEAD_DIM].reshape(1, HEAD_DIM)
 
     barrier = pltpu.get_barrier_semaphore()
 
@@ -185,10 +202,14 @@
 
     def put_query(h, u):
         at = pl.ds(pl.multiple_of(h * HEAD_DIM, HEAD_DIM), HEAD_DIM)
+        to = pl.ds(pl.multiple_of(h * part_rows, part_rows), part_rows)
         u = rope(u + qb_ref[:, at]) * HEAD_DIM ** (-0.5)
-        qt[h] = jnp.transpose(u).astype(BF16)
+        u = jnp.transpose(u).astype(BF16)
+        qt[0, :, to] = u[:, :part_rows]
+        qt[1, :, to] = u[:, part_rows:]
 
     loads[3].wait()
+    loads[4].start()
 
     def query_pair(j, carry):
         at = pl.ds(pl.multiple_of(j * 2 * HEAD_DIM, 2 * HEAD_DIM), 2 * HEAD_DIM)
@@ -201,36 +222,32 @@
     if heads % 2:
         put_query(heads - 1, dot(normed[...], wq[:, (heads - 1) * HEAD_DIM :]))
 
-    def attend(blocks, first):
-        def per_head(h, carry):
-            query = qt[h]
-            scores = []
-            for b in blocks:
-                s = dot(kbuf[b], query)
-                key_at = b * rows + lax.broadcasted_iota(jnp.int32, (rows, 1), 0)
-                scores.append(jnp.where(key_at < limit, s, LOW))
+    m_ref[...] = jnp.full(m_ref.shape, LOW, F32)
+    l_ref[...] = jnp.zeros(l_ref.shape, F32)
+    acc_ref[...] = jnp.zeros(acc_ref.shape, F32)
+    lanes = heads * part_rows
+    tiles = [(t, min(256, lanes - t)) for t in range(0, lanes, 256)]
+
+    def attend(part, blocks):
+        row_at = lax.broadcasted_iota(jnp.int32, (rows, 1), 0)
+        live = [b * rows + row_at < limit for b in blocks]
+        for t, wide in tiles:
+            at = slice(t, t + wide)
+            query = qt[part, :, at]
+            scores = [jnp.where(ok, dot(kbuf[b], query), LOW) for b, ok in zip(blocks, live)]
             tops = [jnp.max(s, axis=0, keepdims=True) for s in scores]
-            top = functools.reduce(jnp.maximum, tops)
-            if not first:
-                old = m_ref[h][:1]
-                top = jnp.maximum(old, top)
-                alpha = jnp.exp(old - top)
-            total, mixed = None, None
+            old = m_ref[part, :, at][:1]
+            top = functools.reduce(jnp.maximum, tops, old)
+            alpha = jnp.exp(old - top)
+            total = l_ref[part, :, at][:1] * alpha
+            mixed = acc_ref[part, :, at] * alpha
             for b, s in zip(blocks, scores):
                 p = jnp.exp(s - top)
-                part = jnp.sum(p, axis=0, keepdims=True)
-                prod = dot(vbuf[b], p.astype(BF16))
-                total = part if total is None else total + part
-                mixed = prod if mixed is None else mixed + prod
-            if not first:
-                total = total + l_ref[h][:1] * alpha
-                mixed = mixed + acc_ref[h] * alpha
-            m_ref[h] = jnp.broadcast_to(top, (8, rows))
-            l_ref[h] = jnp.broadcast_to(total, (8, rows))
-            acc_ref[h] = mixed
-            return carry
-
-        lax.fori_loop(0, heads, per_head, 0)
+                total = total + jnp.sum(p, axis=0, keepdims=True)
+                mixed = mixed + dot(vbuf[b], p.astype(BF16))
+            m_ref[part, :, at] = jnp.broadcast_to(top, (8, wide))
+            l_ref[part, :, at] = jnp.broadcast_to(total, (8, wide))
+            acc_ref[part, :, at] = mixed
 
     def forward(s, kinds_ways):
         for kind in (0, 1):
@@ -242,38 +259,38 @@
     every = ((0, 0), (0, 1), (1, 0), (1, 1))
     last = ((0, 0), (1, 1))
     forward(1, every if half > 2 else last)
-    attend([ms], True)
-    attend([slot(pos - 1), slot(pos + 1)], False)
+    attend(0, [ms])
+    attend(0, [slot(pos - 1), slot(pos + 1)])
 
     def ring_step(s, carry):
         forward(s, every)
-        attend([slot(pos - s), slot(pos + s)], False)
+        attend(0, [slot(pos - s), slot(pos + s)])
         return carry
 
     if half > 3:
         lax.fori_loop(2, half - 1, ring_step, 0)
     if half > 2:
         forward(half - 1, last)
-        attend([slot(pos - half + 1), slot(pos + half - 1)], False)
+        attend(0, [slot(pos - half + 1), slot(pos + half - 1)])
     for way, kind in last:
         arrival(way, kind, half).wait_recv()
-    attend([slot(pos - half)], False)
-
-    def finish(h, carry):
-        at = pl.ds(pl.multiple_of(h * HEAD_DIM, HEAD_DIM), HEAD_DIM)
-        att[:, at] = jnp.transpose(acc_ref[h] / l_ref[h][:1]).astype(BF16)
-        return carry
-
-    lax.fori_loop(0, heads, finish, 0)
+    attend(0, [slot(pos - half)])
+
+    def finish(part):
+        for h in range(heads):
+            at = slice(h * part_rows, (h + 1) * part_rows)
+            done = jnp.transpose(acc_ref[part, :, at] / l_ref[part, :, at][:1]).astype(BF16)
+            cols = slice(h * HEAD_DIM, (h + 1) * HEAD_DIM)
+            att[part * part_rows : (part + 1) * part_rows, cols] = done
 
     loads[4].wait()
     my = lax.div(mh, 2)
     mc = mh - 2 * my
     partner = 2 * my + 1 - mc
 
-    def partial(dest, at, wide):
+    def partial(part, dest, at, wide):
         cols = pl.ds(pl.multiple_of(dest * share + at, HEAD_DIM), wide)
-        return dot(att[...], wo[:, cols])
+        return dot(att[part * part_rows : (part + 1) * part_rows, :], wo[:, cols])
 
     def pair_copy(i):
         return pltpu.make_async_remote_copy(
@@ -296,12 +313,12 @@
         )
 
     def to_partner(i):
-        at, wide = chunks[i]
+        part, at, wide = chunks[i]
         for y in range(n_y):
-            psend[i][y] = partial(2 * y + 1 - mc, at, wide).astype(BF16)
+            psend[i][y] = partial(part, 2 * y + 1 - mc, at, wide).astype(BF16)
         pair_copy(i).start()
         for d in range(1, n_y):
-            pown[i][d] = partial(2 * lax.rem(my + d, n_y) + mc, at, wide)
+            pown[i][d] = partial(part, 2 * lax.rem(my + d, n_y) + mc, at, wide)
 
     def across(i):
         pair_copy(i).wait_recv()
@@ -310,27 +327,44 @@
             ysend[i][d - 1] = (pown[i][d] + precv[i][y].astype(F32)).astype(BF16)
             cross_copy(i, d).start()
 
-    for i in range(len(chunks)):
+    early = [i for i, c in enumerate(chunks) if c[0] == 0]
+    late = [i for i, c in enumerate(chunks) if c[0] == 1]
+    finish(0)
+    for i in early:
         to_partner(i)
-        if i:
+    attend(1, [0, 1])
+    for i in early:
+        across(i)
+
+    def whole_step(i, carry):
+        attend(1, [2 * i, 2 * i + 1])
+        return carry
+
+    lax.fori_loop(1, half, whole_step, 0)
+    finish(1)
+    for i in late:
+        to_partner(i)
+        if i > late[0]:
             across(i - 1)
-    across(len(chunks) - 1)
-    for i, (at, wide) in enumerate(chunks):
-        pown[i][0] = partial(mh, at, wide)
-
-    squares = None
-    outs = []
-    for i, (at, wide) in enumerate(chunks):
+    across(late[-1])
+    for i, (part, at, wide) in enumerate(chunks):
+        pown[i][0] = partial(part, mh, at, wide)
+
+    squares = [None, None]
+    for i, (part, at, wide) in enumerate(chunks):
         mine = pl.ds(pl.multiple_of(mh * share + at, HEAD_DIM), wide)
-        base = tok[:, mine].astype(F32) + (pown[i][0] + precv[i][my].astype(F32))
+        band = slice(part * part_rows, (part + 1) * part_rows)
+        base = tok[band, mine].astype(F32) + (pown[i][0] + precv[i][my].astype(F32))
         for d in range(1, n_y):
             cross_copy(i, d).wait_recv()
             base = base + yrecv[i][d - 1].astype(F32)
-        hid[:, at : at + wide] = base
-        hid_bf[:, at : at + wide] = base.astype(BF16)
+        hid[band, at : at + wide] = base
+        hid_bf[band, at : at + wide] = base.astype(BF16)
         for g in range(0, wide, HEAD_DIM):
             piece = base[:, g : g + HEAD_DIM]
-            squares = piece * piece if squares is None else squares + piece * piece
+            more = piece * piece
+            squares[part] = more if squares[part] is None else squares[part] + more
+    squares = jnp.concatenate(squares, axis=0)
     out_copy = pltpu.make_async_copy(hid_bf, hidden_hbm, local_sem.at[5])
     out_copy.start()
 
@@ -410,7 +444,7 @@
     total = head_sum(wbuf, pow_send, pow_recv, jnp.sum(mean * mean, axis=0, keepdims=True))
     pooled = mean * lax.rsqrt(jnp.sum(total, axis=1, keepdims=True) / width + EPS)
     for g in range(share // HEAD_DIM):
-        emb_ref[:, g * HEAD_DIM : (g + 1) * HEAD_DIM] = pooled[g : g + 1]
+        emb_ref[g * HEAD_DIM : (g + 1) * HEAD_DIM] = pooled[g : g + 1].reshape(HEAD_DIM)
 
     def sent(s, carry):
         for way, kind in every:
@@ -465,13 +499,13 @@
     chunks = widths(share)
     groups = -(-share // (8 * HEAD_DIM)) * 8
     chunk_bufs = []
-    for _, wide in chunks:
+    for _, _, wide in chunks:
         chunk_bufs += [
-            pltpu.VMEM((n_y, rows, wide), BF16),
-            pltpu.VMEM((n_y, rows, wide), BF16),
-            pltpu.VMEM((n_y, rows, wide), F32),
-            pltpu.VMEM((n_y - 1, rows, wide), BF16),
-            pltpu.VMEM((n_y - 1, rows, wide), BF16),
+            pltpu.VMEM((n_y, rows // 2, wide), BF16),
+            pltpu.VMEM((n_y, rows // 2, wide), BF16),
+            pltpu.VMEM((n_y, rows // 2, wide), F32),
+            pltpu.VMEM((n_y - 1, rows // 2, wide), BF16),
+            pltpu.VMEM((n_y - 1, rows // 2, wide), BF16),
         ]
     dma = pltpu.SemaphoreType.DMA
     hbm = pl.BlockSpec(memory_space=pl.ANY)
@@ -481,11 +515,16 @@
         functools.partial(kernel, n_seq, n_head),
         out_shape=(
             jax.ShapeDtypeStruct((rows, share), BF16),
-            jax.ShapeDtypeStruct((1, share), F32),
+            jax.ShapeDtypeStruct((share,), F32),
         ),
         in_specs=[smem, hbm, vmem, hbm, vmem, hbm, vmem, hbm, vmem, hbm] + [vmem] * 5,
         out_specs=(hbm, vmem),
         scratch_shapes=[
+            pltpu.VMEM((1, width), F32),
+            pltpu.VMEM((1, heads * HEAD_DIM), F32),
+            pltpu.VMEM((1, HEAD_DIM), F32),
+            pltpu.VMEM((1, HEAD_DIM), F32),
+            pltpu.VMEM((1, share), F32),
             pltpu.VMEM((rows, width), BF16),
             pltpu.VMEM((rows, width), BF16),
             pltpu.VMEM((width, 2 * HEAD_DIM), BF16),
@@ -493,12 +532,12 @@
             pltpu.VMEM(o_weight.shape, BF16),
             pltpu.VMEM((rows, HEAD_DIM), F32),
             pltpu.VMEM((rows, HEAD_DIM), F32),
-            pltpu.VMEM((heads, HEAD_DIM, rows), BF16),
+            pltpu.VMEM((2, HEAD_DIM, heads * (rows // 2)), BF16),
             pltpu.VMEM((n_seq, rows, HEAD_DIM), BF16),
             pltpu.VMEM((n_seq, HEAD_DIM, rows), BF16),
-            pltpu.VMEM((heads, 8, rows), F32),
-            pltpu.VMEM((heads, 8, rows), F32),
-            pltpu.VMEM((heads, HEAD_DIM, rows), F32),
+            pltpu.VMEM((2, 8, heads * (rows // 2)), F32),
+            pltpu.VMEM((2, 8, heads * (rows // 2)), F32),
+            pltpu.VMEM((2, HEAD_DIM, heads * (rows // 2)), F32),
             pltpu.VMEM((rows, heads * HEAD_DIM), BF16),
             pltpu.VMEM((rows, share), F32),
             pltpu.VMEM((rows, share), BF16),
@@ -526,18 +565,18 @@
     )(
         length,
         tokens,
-        in_gain[None, :],
+        in_gain,
         q_weight,
-        q_bias[None, :],
+        q_bias,
         k_weight,
-        k_bias[None, :],
+        k_bias,
         v_weight,
-        v_bias[None, :],
+        v_bias,
         o_weight,
-        final_gain[None, :],
+        final_gain,
         *tables,
     )
-    return hidden, embedding[0]
+    return hidden, embedding
 
 
 def solution(mesh):

time: 65.7 us -> 56.9 us (0.87)
  Pallas kernels: 57.1 us -> 52.3 us
  local copies, waits for them, and re-layouts: 5.69 us -> 3.09 us
  other arithmetic: 1.29 us -> 0 us
    pallas_call x1, Pallas kernels: 57.1 us -> 52.3 us  [body(): pl.pallas_call(functools.partial(kernel, n_seq, n_head), out_shape=(jax.S...]
    broadcast_in_dim x3 -> x0, local copies, waits for them, and re-layouts: 3.87 us -> none  [the longest x1 1.33 us: body(): in_gain[None, :]]
    pallas_call x1 -> x0, other arithmetic: 1.29 us -> none  [body(): pl.pallas_call(functools.partial(kernel, n_seq, n_head), out_shape=(jax.S...]
    unnamed x1 -> x2, local copies, waits for them, and re-layouts: 1.82 us -> 3.09 us
where the time goes in v2:
time: 56.9 us; the launch traced here: 56.6 us
  Pallas kernels  52.3 us (92%)
  local copies, waits for them, and re-layouts  3.09 us (5%)
  between operations  1.29 us (2%)
    pallas_call x1, Pallas kernels, body(): pl.pallas_call(functools.partial(kernel, n_seq, n_head), out_shape=(jax.S...  52.3 us
    unnamed x2, local copies, waits for them, and re-layouts  3.09 us

profile of v2, /device:TPU:0, one launch (start us, length us, event | category | flops | bytes accessed | tf_op | source)
XLA Modules:
  0.0 56.6 jit_solution(8124690687570446369)
XLA Ops:
  1.3 52.3 %shard_map.158 = (bf16[256,896]{1,0:T(8,128)(2,1)}, f32[896]{0:T(1024)}) custom-call(s32[1]{0:T(128)S(6)} %copy.19.length_ref, bf16[256,3584]{1,0:T(8,128)(2,1)} %tokens_hbm.1, f32[3584]{0:T(1024)} %gain_1d.1, bf16[3584,896]{1,0:T(8,128)(2,1)} %wq_hbm.1, f32[896]{0:T(1024)} %qb_1d.1, bf16[3584,128]{1,0:T(8,128)(2,1)} %wk_hbm.1, f32[128]{0:T(128)} %kb_1d.1, ...), custom_call_target="tpu_custom_call" | custom-call | tf_op jit(solution)/shard_map/pallas_call | solution.py:514
  53.5 1.8 %copy.20 = bf16[256,896]{1,0:T(8,128)(2,1)} copy(bf16[256,896]{1,0:T(8,128)(2,1)} %get-tuple-element.4) | data formatting | bytes 917504
  55.4 1.3 %copy.21 = f32[896]{0:T(1024)} copy(f32[896]{0:T(1024)} %get-tuple-element.5) | data formatting | bytes 7168
